TPU v7x, 256 devices: a whole 4x4x8 slice. The times are simulated.
256 devices in a mesh: seq: 32 (over x, z), batch: 8 (over y, core).
Axes of the slice: x: 4, y: 4, z: 8, core: 2. Of those that a mesh axis runs over, the one named last changes fastest.
Arguments:
- hidden: bfloat16 [16, 8192, 4096], P('batch', None, 'seq')
- gain: float32 [4096], P('seq'), may hold values from 0.5 to 1.5
- value_weight: float32 [4096], P('seq'), may hold values from -0.09375 to 0.09375
- rewards: float32 [16, 8192], P('batch', 'seq'), may hold values from -1.5 to 1.5
- reward_mask: int32 [16, 8192], P('batch', 'seq'), may hold values 0 or 1
- lengths: int32 [16], P('batch'), may hold values from 2048 to 8192
- horizon: float32 [16], P('batch'), may hold values from 24 to 65536
Outputs:
- advantages: float32 [16, 8192], P(None, ('seq', 'batch'))
- returns: float32 [16, 8192], P(None, ('seq', 'batch'))
All inputs are finite; a program needn't handle non-finite values. No bound on the sum of `reward_mask` on one device may be relied on, other than what follows from the above.
Results may differ from a plain program's by a relative error of at most 0.0003.
Values may be sent and summed in bfloat16 or wider, within the bound.
A program may use at most 64 MiB of HBM per device.

v0:
```python
import jax
import jax.numpy as jnp
from jax import lax
from jax.sharding import Mesh
from jax.sharding import PartitionSpec as P

D = 4096
SEQ = ("seq_0", "seq_1")
SEQ_BATCH = ("seq_0", "seq_1", "batch_0", "batch_1")
BATCH = ("batch_0", "batch_1")


EPS = 1e-05


def cut_along(array, dim, devices):
    dims = array.shape
    blocks = array.reshape(*dims[:dim], devices, dims[dim] // devices, *dims[dim + 1 :])
    return jnp.moveaxis(blocks, dim, 0)


def sent_and_summed(array, axis, dim):
    devices = lax.axis_size(axis)
    blocks = lax.all_to_all(cut_along(array, dim, devices), axis, 0, 0, tiled=True)
    return jnp.sum(blocks, axis=0)


def side_by_side(arrays, axis, dim, along):
    widths = [a.shape[along] for a in arrays]
    both = jnp.concatenate(arrays, axis=along)
    whole = sent_and_summed(both, axis, dim)
    return tuple(jnp.split(whole, [sum(widths[:k]) for k in range(1, len(widths))], axis=along))


def from_behind(value, axis, steps):
    count = lax.axis_size(axis)
    initial, last = (max(0, -steps), min(count, count - steps))
    return lax.ppermute(value, axis, [(source, source + steps) for source in range(initial, last)])


def sent_to_all(array, axis):
    devices = lax.axis_size(axis)
    return lax.all_to_all(
        jnp.broadcast_to(array[None], (devices, *array.shape)), axis, 0, 0, tiled=True
    )


def gathered_once(array, axis):
    leaves = jax.tree.leaves(array)
    turns = sorted(range(len(leaves)), key=lambda k: -leaves[k].size)
    width = (1, *leaves[turns[0]].shape)[-1]
    lines = [
        jnp.pad(leaves[k].reshape(-1), (0, -leaves[k].size % width)).reshape(-1, width)
        for k in turns
    ]
    both, at, found = (sent_to_all(jnp.concatenate(lines), axis), 0, {})
    for k, line in zip(turns, lines):
        slab = both[:, at : at + len(line)].reshape(len(both), -1)
        found[k] = slab[:, : leaves[k].size].reshape(-1, *leaves[k].shape)
        at += len(line)
    numbers = iter(range(len(leaves)))
    return jax.tree.map(lambda _: found[next(numbers)], array)


def joined_by_halves(pieces, combine):
    while len(jax.tree.leaves(pieces)[0]) > 1:
        pieces = jax.vmap(combine)(
            *(jax.tree.map(lambda part: part[side::2], pieces) for side in (0, 1))
        )
    return jax.tree.map(lambda part: part[0], pieces)


def prefix(array, axis, combine, identity):
    devices, position = (lax.axis_size(axis), lax.axis_index(axis))
    passed = jnp.arange(devices) > position

    def kept(part, zero, own):
        part = jnp.where(
            passed.reshape(-1, *(1 for _ in own.shape)), part, jnp.asarray(zero, own.dtype)
        )
        return part[::-1]

    pieces = gathered_once(array, axis)
    return joined_by_halves(jax.tree.map(kept, pieces, identity, array), combine)


def one_axis_at_a_time(array, axes):
    for axis in axes:
        array = lax.psum(array, axis)
    return array


def per_device(hidden, gain, value_weight, rewards, reward_mask, lengths, horizon):
    my_index = lax.axis_index(SEQ)
    block = rewards.shape[1]
    wide_rows = hidden.astype(jnp.float32)
    part_squares = jnp.sum(wide_rows * wide_rows, -1)
    part_projected = jnp.sum(wide_rows * (gain * value_weight), -1)
    squares, projected = side_by_side((part_squares, part_projected), SEQ, 1, 0)
    values = projected * lax.rsqrt(squares / D + EPS)
    positions = my_index * block + jnp.arange(block, dtype=jnp.int32)
    valid = (positions[None, :] < lengths[:, None]).astype(jnp.float32)
    next_valid = (positions[None, :] + 1 < lengths[:, None]).astype(jnp.float32)
    following = from_behind(values[:, 0], SEQ, -1)
    next_values = jnp.concatenate([values[:, 1:], following[:, None]], 1)
    delta = (rewards * reward_mask.astype(jnp.float32) + next_valid * next_values - values) * valid
    log_decay = -1.0 / horizon
    offsets = jnp.arange(block, dtype=jnp.int32)
    distance = (offsets[None, :] - offsets[:, None]).astype(jnp.float32)
    upper_mask = distance >= 0.0
    powers = jnp.where(
        upper_mask[None], jnp.exp(jnp.maximum(distance, 0.0)[None] * log_decay[:, None, None]), 0.0
    )
    local_gae = jnp.einsum("rtk,rk->rt", powers, delta, precision=lax.Precision.HIGHEST)
    tail_decay = jnp.exp((block - offsets).astype(jnp.float32)[None, :] * log_decay[:, None])
    start_value = local_gae[:, 0]
    block_decay = jnp.exp(block * log_decay)

    def compose(earlier, later):
        return (later[0] + later[1] * earlier[0], later[1] * earlier[1])

    carry_in, _ = prefix(
        (start_value, block_decay),
        SEQ,
        compose,
        (jnp.zeros_like(start_value), jnp.ones_like(block_decay)),
    )
    gae = local_gae + tail_decay * carry_in[:, None]
    returns = (gae + values) * valid
    count, first, second = (
        one_axis_at_a_time(jnp.sum(valid), SEQ_BATCH),
        one_axis_at_a_time(jnp.sum(gae), SEQ_BATCH),
        one_axis_at_a_time(jnp.sum(gae * gae), SEQ_BATCH),
    )
    mean = first / count
    var = jnp.maximum(second / count - mean * mean, 1.0)
    whitened = (gae - mean) * valid * lax.rsqrt(var)
    out_adv, out_returns = (
        lax.all_to_all(whitened, BATCH, split_axis=1, concat_axis=0, tiled=True),
        lax.all_to_all(returns, BATCH, split_axis=1, concat_axis=0, tiled=True),
    )
    return (out_adv, out_returns)


def solution(mesh):
    finer = Mesh(mesh.devices.reshape(4, 8, 4, 2), ("seq_0", "seq_1", "batch_0", "batch_1"))
    placed = (P(BATCH, None, SEQ), P(SEQ), P(SEQ), P(BATCH, SEQ), P(BATCH, SEQ), P(BATCH), P(BATCH))
    return jax.shard_map(
        per_device,
        mesh=finer,
        in_specs=placed,
        out_specs=(P(None, SEQ_BATCH), P(None, SEQ_BATCH)),
        check_vma=False,
    )
```

profile of v0, /device:TPU:1, one launch (start us, length us, event | category | flops | bytes accessed | tf_op | source)
XLA Modules:
  0.0 118.5 jit_solution(17248735630217335933)
XLA Ops:
  0.7 0.7 mul.124
  1.4 6.7 %fusion = (f32[2,8192]{1,0:T(2,128)S(1)}, f32[2,8192]{1,0:T(2,128)S(1)}) fusion(bf16[2,8192,128]{2,1,0:T(8,128)(2,1)} %param.7, f32[128]{0:T(128)S(1)} %mul.124), kind=kLoop, calls=%fused_computation.2 | loop fusion | flops 10452992 | bytes 4325888 | tf_op jit(solution)/shard_map/reduce_sum | solution.py:97
  8.0 0.7 pad_maximum_fusion
  8.7 11.9 %all-to-all-start = ((f32[32,4,256]{2,1,0:T(4,128)}), f32[32,4,256]{2,1,0:T(4,128)S(1)}, u32[]{:S(2)}, u32[]{:S(2)}) async-start(f32[32,4,256]{2,1,0:T(4,128)} %bitcast.1), calls=%async_computation | async-start | bytes 262144 | tf_op jit(solution)/shard_map/all_to_all | solution.py:24
  20.8 9.0 %all-to-all-done = f32[32,4,256]{2,1,0:T(4,128)S(1)} async-done(((f32[32,4,256]{2,1,0:T(4,128)}), f32[32,4,256]{2,1,0:T(4,128)S(1)}, u32[]{:S(2)}, u32[]{:S(2)}) %all-to-all-start) | async-done | bytes 131104 | tf_op jit(solution)/shard_map/all_to_all | solution.py:24
  29.8 0.1 slice_reduce_fusion.1
  30.0 1.3 %collective-permute-start = (f32[2]{0:T(128)S(1)}, f32[2]{0:T(128)S(1)}, u32[]{:S(2)}, u32[]{:S(2)}) collective-permute-start(f32[2]{0:T(128)S(1)} %slice_reduce_fusion.1), channel_id=1, source_target_pairs={{8,0},{16,8},{24,16},{32,24},{40,32},{48,40},{56,48},{64,56},{72,6... | collective-permute-start | bytes 32 | tf_op jit(solution)/shard_map/ppermute | solution.py:38
  31.3 3.0 %collective-permute-done = f32[2]{0:T(128)S(1)} collective-permute-done((f32[2]{0:T(128)S(1)}, f32[2]{0:T(128)S(1)}, u32[]{:S(2)}, u32[]{:S(2)}) %collective-permute-start) | collective-permute-done | bytes 40 | tf_op jit(solution)/shard_map/ppermute | solution.py:38
  34.5 0.7 fusion.2
  35.2 0.1 slice_reduce_fusion
  35.3 0.6 broadcast_in_dim.55
  35.9 5.2 %all-to-all-start.1 = ((f32[32,2,2]{2,1,0:T(2,128)}), f32[32,2,2]{2,1,0:T(2,128)S(1)}, u32[]{:S(2)}, u32[]{:S(2)}) async-start(f32[32,2,2]{2,1,0:T(2,128)} %broadcast_in_dim.55), calls=%async_computation.1 | async-start | bytes 65536 | tf_op jit(solution)/shard_map/all_to_all | solution.py:43
  41.1 8.8 %all-to-all-done.1 = f32[32,2,2]{2,1,0:T(2,128)S(1)} async-done(((f32[32,2,2]{2,1,0:T(2,128)}), f32[32,2,2]{2,1,0:T(2,128)S(1)}, u32[]{:S(2)}, u32[]{:S(2)}) %all-to-all-start.1) | async-done | bytes 544 | tf_op jit(solution)/shard_map/all_to_all | solution.py:43
  50.1 0.1 slice.99
  50.2 0.1 slice.94
  50.3 0.1 slice.91
  50.4 0.1 slice.96
  52.1 0.2 add_reduce_fusion
  52.3 0.7 compare_select_fusion
  53.0 0.6 fusion.20
  53.6 7.6 %all-reduce.2 = (f32[]{:T(128)}, f32[]{:T(128)}, f32[]{:T(128)}) all-reduce(f32[]{:T(128)} %get-tuple-element.5, f32[]{:T(128)} %get-tuple-element.24, f32[]{:T(128)} %get-tuple-element.4), channel_id=1, replica_groups=mesh['seq_0'=4,'seq_1'=8,'batch_0'=4,'batch_1'=2] {'seq_0'}, use_global_device_ids=true, to_apply=%region_14.15 | all-reduce | flops 3 | bytes 24 | tf_op jit(solution)/shard_map/psum | solution.py:89
  61.1 11.8 %all-reduce = (f32[]{:T(128)}, f32[]{:T(128)}, f32[]{:T(128)}) all-reduce(f32[]{:T(128)} %get-tuple-element.12, f32[]{:T(128)} %get-tuple-element.13, f32[]{:T(128)} %get-tuple-element.14), channel_id=1, replica_groups=mesh['seq_0'=4,'seq_1'=8,'batch_0'=4,'batch_1'=2] {'seq_1'}, use_global_device_ids=true, to_apply=%region_15.16 | all-reduce | flops 3 | bytes 24 | tf_op jit(solution)/shard_map/psum | solution.py:89
  72.9 9.7 %all-reduce.1 = (f32[]{:T(128)}, f32[]{:T(128)}, f32[]{:T(128)}) all-reduce(f32[]{:T(128)} %get-tuple-element.6, f32[]{:T(128)} %get-tuple-element.7, f32[]{:T(128)} %get-tuple-element.8), channel_id=1, replica_groups=mesh['seq_0'=4,'seq_1'=8,'batch_0'=4,'batch_1'=2] {'batch_0'}, use_global_device_ids=true, to_apply=%region_16.17 | all-reduce | flops 3 | bytes 24 | tf_op jit(solution)/shard_map/psum | solution.py:89
  82.6 14.5 %all-reduce.3 = (f32[]{:T(128)}, f32[]{:T(128)}, f32[]{:T(128)}) all-reduce(f32[]{:T(128)} %get-tuple-element.9, f32[]{:T(128)} %get-tuple-element.10, f32[]{:T(128)} %get-tuple-element.11), channel_id=1, replica_groups=mesh['seq_0'=4,'seq_1'=8,'batch_0'=4,'batch_1'=2] {'batch_1'}, use_global_device_ids=true, to_apply=%region_17.18 | all-reduce | flops 3 | bytes 24 | tf_op jit(solution)/shard_map/psum | solution.py:89
  99.9 0.6 copy.18
  100.6 3.6 %all-to-all-start.2 = ((f32[2,8,32]{2,0,1:T(2,128)}), f32[2,8,32]{2,0,1:T(2,128)S(1)}, u32[]{:S(2)}, u32[]{:S(2)}) async-start(f32[2,8,32]{2,0,1:T(2,128)} %copy.18), calls=%async_computation.2 | async-start | bytes 16384 | tf_op jit(solution)/shard_map/all_to_all | solution.py:139
  104.2 0.6 copy.19
  104.8 4.0 %all-to-all-done.2 = f32[2,8,32]{2,0,1:T(2,128)S(1)} async-done(((f32[2,8,32]{2,0,1:T(2,128)}), f32[2,8,32]{2,0,1:T(2,128)S(1)}, u32[]{:S(2)}, u32[]{:S(2)}) %all-to-all-start.2) | async-done | bytes 2080 | tf_op jit(solution)/shard_map/all_to_all | solution.py:139
  108.8 3.9 %all-to-all-start.3 = ((f32[2,8,32]{2,0,1:T(2,128)}), f32[2,8,32]{2,0,1:T(2,128)S(1)}, u32[]{:S(2)}, u32[]{:S(2)}) async-start(f32[2,8,32]{2,0,1:T(2,128)} %copy.19), calls=%async_computation.3 | async-start | bytes 16384 | tf_op jit(solution)/shard_map/all_to_all | solution.py:140
  112.7 4.6 %all-to-all-done.3 = f32[2,8,32]{2,0,1:T(2,128)S(1)} async-done(((f32[2,8,32]{2,0,1:T(2,128)}), f32[2,8,32]{2,0,1:T(2,128)S(1)}, u32[]{:S(2)}, u32[]{:S(2)}) %all-to-all-start.3) | async-done | bytes 2080 | tf_op jit(solution)/shard_map/all_to_all | solution.py:140
  117.4 0.6 copy.31
  118.0 0.6 copy.32
  (48 shorter events, 2.4 us)
Async XLA Ops:
  0.6 20.1 %copy-start.3 = (f32[2]{0:T(128)S(1)}, f32[2]{0:T(128)}, u32[]{:S(2)}) copy-start(f32[2]{0:T(128)} %param.13) | copy-start | bytes 28
  0.6 33.8 %copy-start.1 = (f32[2,256]{1,0:T(2,128)S(1)}, f32[2,256]{1,0:T(2,128)}, u32[]{:S(2)}) copy-start(f32[2,256]{1,0:T(2,128)} %param.10) | copy-start | bytes 6148
  0.7 33.7 %copy-start.2 = (s32[2,256]{1,0:T(2,128)S(1)}, s32[2,256]{1,0:T(2,128)}, u32[]{:S(2)}) copy-start(s32[2,256]{1,0:T(2,128)} %param.11) | copy-start | bytes 6148
  0.7 33.7 %copy-start = (s32[2]{0:T(128)S(1)}, s32[2]{0:T(128)}, u32[]{:S(2)}) copy-start(s32[2]{0:T(128)} %param.12) | copy-start | bytes 28
  8.7 21.0 %all-to-all-start = ((f32[32,4,256]{2,1,0:T(4,128)}), f32[32,4,256]{2,1,0:T(4,128)S(1)}, u32[]{:S(2)}, u32[]{:S(2)}) async-start(f32[32,4,256]{2,1,0:T(4,128)} %bitcast.1), calls=%async_computation | async-start | bytes 262144 | tf_op jit(solution)/shard_map/all_to_all | solution.py:24
  30.0 4.3 %collective-permute-start = (f32[2]{0:T(128)S(1)}, f32[2]{0:T(128)S(1)}, u32[]{:S(2)}, u32[]{:S(2)}) collective-permute-start(f32[2]{0:T(128)S(1)} %slice_reduce_fusion.1), channel_id=1, source_target_pairs={{8,0},{16,8},{24,16},{32,24},{40,32},{48,40},{56,48},{64,56},{72,6... | collective-permute-start | bytes 32 | tf_op jit(solution)/shard_map/ppermute | solution.py:38
  35.9 13.9 %all-to-all-start.1 = ((f32[32,2,2]{2,1,0:T(2,128)}), f32[32,2,2]{2,1,0:T(2,128)S(1)}, u32[]{:S(2)}, u32[]{:S(2)}) async-start(f32[32,2,2]{2,1,0:T(2,128)} %broadcast_in_dim.55), calls=%async_computation.1 | async-start | bytes 65536 | tf_op jit(solution)/shard_map/all_to_all | solution.py:43
  100.6 8.2 %all-to-all-start.2 = ((f32[2,8,32]{2,0,1:T(2,128)}), f32[2,8,32]{2,0,1:T(2,128)S(1)}, u32[]{:S(2)}, u32[]{:S(2)}) async-start(f32[2,8,32]{2,0,1:T(2,128)} %copy.18), calls=%async_computation.2 | async-start | bytes 16384 | tf_op jit(solution)/shard_map/all_to_all | solution.py:139
  108.8 8.6 %all-to-all-start.3 = ((f32[2,8,32]{2,0,1:T(2,128)}), f32[2,8,32]{2,0,1:T(2,128)S(1)}, u32[]{:S(2)}, u32[]{:S(2)}) async-start(f32[2,8,32]{2,0,1:T(2,128)} %copy.19), calls=%async_computation.3 | async-start | bytes 16384 | tf_op jit(solution)/shard_map/all_to_all | solution.py:140
where the time goes:
time: 119 us
  blocking collectives  43.6 us (37%)
  waiting for transfers between devices  29.4 us (25%)
  starting transfers between devices  25.8 us (22%)
  other arithmetic  9.9 us (8%)
  local copies, waits for them, and re-layouts  5.74 us (5%)
  between operations  3.44 us (3%)
    psum x4, blocking collectives, one_axis_at_a_time(): array = lax.psum(array, axis)  43.6 us
    all_to_all x1, starting transfers between devices, sent_and_summed(): lax.all_to_all(cut_along(array, dim, devices), axis, 0, 0, tiled=True)  11.9 us
    all_to_all x1, waiting for transfers between devices, sent_and_summed(): lax.all_to_all(cut_along(array, dim, devices), axis, 0, 0, tiled=True)  8.98 us
    all_to_all x1, waiting for transfers between devices, sent_to_all(): lax.all_to_all(jnp.broadcast_to(array[None], (devices, *array.shape)), ax...  8.76 us
    reduce_sum x1, other arithmetic, per_device(): part_squares = jnp.sum(wide_rows * wide_rows, -1)  6.65 us
    all_to_all x1, starting transfers between devices, sent_to_all(): lax.all_to_all(jnp.broadcast_to(array[None], (devices, *array.shape)), ax...  5.16 us
    all_to_all x1, waiting for transfers between devices, per_device(): lax.all_to_all(returns, BATCH, split_axis=1, concat_axis=0, tiled=True)  4.64 us
    all_to_all x1, waiting for transfers between devices, per_device(): lax.all_to_all(whitened, BATCH, split_axis=1, concat_axis=0, tiled=True)  3.96 us
  transfers between devices with their start and end apart: 5, of which 5 were waited for; matrix products, arithmetic and copies ran while one was open for 1% of the time, Pallas kernels for 0%

commit v1 on v0

v1 whole, which is shorter than its diff:
```python
import jax
import jax.numpy as jnp
from jax import lax
from jax.experimental import pallas as pl
from jax.experimental.pallas import tpu as pltpu
from jax.sharding import PartitionSpec as P

D = 4096
EPS = 1e-05
NX, NZ = 4, 8
NS = NX * NZ
NB = 8
BLOCK = 256
CHUNKS = 8
PER_CHUNK = NS // CHUNKS
MESH = pl.DeviceIdType.MESH
F32 = jnp.float32
BF16 = jnp.bfloat16


def ring(d, n):
    return min(d, n - d)


OFFSETS = sorted(
    ((dx, dz) for dx in range(NX) for dz in range(NZ) if dx or dz),
    key=lambda o: (-(ring(o[0], NX) + ring(o[1], NZ)), o),
)


def iota(shape, dim):
    return lax.broadcasted_iota(jnp.int32, shape, dim)


def kernel(
    hidden, gain, weight, rewards, mask, lengths, horizon, adv_ref, ret_ref,
    hv, gv, wv, rv, mv, lens, hors, send1, recv1, send2, recv2, send3, recv3,
    hsem, gsem, isem, ssem, rsem,
):
    me, mb = lax.axis_index("seq"), lax.axis_index("batch")
    mx, mz = me // NZ, me % NZ
    span = CHUNKS and hv.shape[1] // CHUNKS

    def chunk_copy(c):
        at = pl.ds(pl.multiple_of(c * span, span), span)
        return pltpu.make_async_copy(hidden.at[:, at], hv.at[:, at], hsem.at[c])

    def peer(dx, dz):
        return lax.rem(mx + dx, NX) * NZ + lax.rem(mz + dz, NZ)

    def batch_peer(k):
        return lax.rem(mb + k, NB)

    weights = [
        pltpu.make_async_copy(gain, gv, gsem.at[0]),
        pltpu.make_async_copy(weight, wv, gsem.at[1]),
    ]
    for copy in weights:
        copy.start()
    for c in range(CHUNKS):
        chunk_copy(c).start()
    smalls = [
        pltpu.make_async_copy(src, dst, isem.at[k])
        for k, (src, dst) in enumerate(
            ((rewards, rv), (mask, mv), (lengths, lens), (horizon, hors))
        )
    ]
    for copy in smalls:
        copy.start()

    barrier = pltpu.get_barrier_semaphore()
    for dx, dz in OFFSETS:
        pl.semaphore_signal(barrier, inc=1, device_id={"seq": peer(dx, dz)}, device_id_type=MESH)
    for k in range(1, NB):
        pl.semaphore_signal(barrier, inc=1, device_id={"batch": batch_peer(k)}, device_id_type=MESH)

    for copy in weights:
        copy.wait()
    head = gv[...].reshape(1, 128) * wv[...].reshape(1, 128)
    high = head.astype(BF16).astype(F32)
    middle = (head - high).astype(BF16).astype(F32)
    low = head - high - middle
    row16 = iota((16, 128), 0)
    left = jnp.where(row16 == 0, high, jnp.where(row16 == 1, middle, jnp.where(row16 == 2, low, 0.0)))
    left = left.astype(BF16)
    ones = jnp.ones((16, 256), BF16)
    row = iota((8, 128), 0)
    lane = iota((8, 128), 1)
    across = (((1,), (1,)), ((), ()))

    def sums_of_chunk(c, _):
        chunk_copy(c).wait()
        for i in range(PER_CHUNK):
            block = c * PER_CHUNK + i
            tile = jnp.zeros((8, 128), F32)
            for r in range(2):
                h = hv[r, pl.ds(pl.multiple_of(block * BLOCK, BLOCK), BLOCK), :]
                wide = h.astype(F32)
                square = wide * wide
                square_high = square.astype(BF16)
                square_low = (square - square_high.astype(F32)).astype(BF16)
                parts = lax.dot_general(left, h, across, preferred_element_type=F32)
                projected = jnp.sum(parts[0:8], axis=0, keepdims=True)
                both = jnp.concatenate([square_high, square_low], axis=1)
                squares = lax.dot_general(ones, both, across, preferred_element_type=F32)[0:8]
                for half in range(2):
                    at = slice(half * 128, half * 128 + 128)
                    k = r * 2 + half
                    tile = jnp.where(row == k, squares[:, at], tile)
                    tile = jnp.where(row == k + 4, projected[:, at], tile)
            send1[block] = tile
        return 0

    lax.fori_loop(0, CHUNKS, sums_of_chunk, 0)

    pl.semaphore_wait(barrier, NS - 1 + NB - 1)

    def first_copy(dx, dz):
        return pltpu.make_async_remote_copy(
            src_ref=send1.at[peer(dx, dz)],
            dst_ref=recv1.at[dx * NZ + dz - 1],
            send_sem=ssem.at[0],
            recv_sem=rsem.at[0],
            device_id={"seq": peer(dx, dz)},
            device_id_type=MESH,
        )

    for dx, dz in OFFSETS:
        first_copy(dx, dz).start()

    for copy in smalls:
        copy.wait()
    resp = (row >> 1) & 1
    half = row & 1
    length = jnp.where(resp == 0, lens[0], lens[1])
    position = me * BLOCK + half * 128 + lane
    valid = (position < length).astype(F32)
    next_valid = (position + 1 < length).astype(F32)
    rate = -1.0 / jnp.where(resp == 0, hors[0], hors[1])
    inside = half * 128 + lane
    steps = [
        jnp.where(lane < 128 - (1 << i), jnp.exp(rate * float(1 << i)), 0.0) for i in range(7)
    ]
    over_half = jnp.where(half == 0, jnp.exp(rate * (128 - lane).astype(F32)), 0.0)
    tail = jnp.exp(rate * (255 - inside).astype(F32))
    reward4 = jnp.concatenate(
        [rv[r : r + 1, h * 128 : h * 128 + 128] * mv[r : r + 1, h * 128 : h * 128 + 128].astype(F32)
         for _ in range(2) for r in range(2) for h in range(2)], axis=0)
    reward4 = reward4 * valid

    def per_response(x):
        both = x + pltpu.roll(x, 7, 0)
        return jnp.sum(both, axis=1, keepdims=True)

    def by_lane(column):
        wide = jnp.broadcast_to(column, (8, 128))
        return jnp.where(lane[0:1] < 64, wide[0:1], wide[2:3])

    tails = by_lane(per_response(tail))
    tails2 = by_lane(per_response(tail * tail))
    lane32 = iota((NS, 128), 1)
    j = iota((NS, 128), 0)
    rate32 = -1.0 / jnp.where(lane32 < 64, hors[0], hors[1])
    length32 = jnp.where(lane32 < 64, lens[0], lens[1])
    more = ((j + 1) * BLOCK < length32).astype(F32)
    block_steps = [
        jnp.where(j < NS - (1 << i), jnp.exp(rate32 * float(BLOCK << i)), 0.0) for i in range(5)
    ]
    to_start = jnp.exp(rate32 * float(BLOCK - 1)) * more
    once = jnp.where(j < NS - 1, jnp.exp(rate32), 0.0)

    def arrived(buffer, count, sem):
        whole = buffer.at[pl.ds(0, count)]
        pltpu.make_async_remote_copy(
            src_ref=whole, dst_ref=whole, send_sem=ssem.at[0], recv_sem=sem,
            device_id={"seq": peer(0, 1)}, device_id_type=MESH,
        ).wait_recv()

    arrived(recv1, NS - 1, rsem.at[0])
    total = send1[me] + jnp.sum(recv1[...], axis=0)
    other = pltpu.roll(total, 4, 0)
    squares = jnp.where(row < 4, total, other)
    projected = jnp.where(row < 4, other, total)
    values = projected * lax.rsqrt(squares * (1.0 / D) + EPS)
    following = pltpu.roll(values, 127, 1)
    following = jnp.where(
        lane == 127, jnp.where(half == 0, pltpu.roll(following, 7, 0), 0.0), following
    )
    x = reward4 + (next_valid * following - values) * valid
    for i in range(7):
        x = x + steps[i] * pltpu.roll(x, 128 - (1 << i), 1)
    x = x + over_half * jnp.broadcast_to(pltpu.roll(x, 7, 0)[:, 0:1], (8, 128))

    columns = (
        x[:, 0:1], values[:, 0:1], per_response(x), per_response(x * x), per_response(x * tail)
    )
    packed = jnp.zeros((8, 128), F32)
    for k, column in enumerate(columns):
        packed = jnp.where((lane & 63) == k, column, packed)
    message = jnp.where(lane[0:1] < 64, packed[0:1], packed[2:3])
    send2[...] = message
    recv2[me] = message

    def second_copy(dx, dz):
        return pltpu.make_async_remote_copy(
            src_ref=send2,
            dst_ref=recv2.at[me],
            send_sem=ssem.at[1],
            recv_sem=rsem.at[1],
            device_id={"seq": peer(dx, dz)},
            device_id_type=MESH,
        )

    for dx, dz in OFFSETS:
        second_copy(dx, dz).start()
    arrived(recv2, NS - 1, rsem.at[1])

    start = recv2[...].reshape(NS, 128)
    first_value, sum1, sum2, cross = (pltpu.roll(start, 128 - k, 1) for k in range(1, 5))
    next_first = pltpu.roll(first_value, NS - 1, 0)
    g = start + to_start * next_first
    for i in range(5):
        g = g + block_steps[i] * pltpu.roll(g, NS - (1 << i), 0)
    carry = once * pltpu.roll(g, NS - 1, 0) + more * next_first
    first = jnp.sum(sum1 + carry * tails, axis=0, keepdims=True)
    second = jnp.sum(sum2 + carry * (2.0 * cross + carry * tails2), axis=0, keepdims=True)
    mine = jnp.sum(jnp.where(j == me, carry, 0.0), axis=0, keepdims=True)
    gae = x + tail * jnp.where(resp == 0, mine[:, 0:1], mine[:, 64:65])
    returns = (gae + values) * valid
    tokens = (lens[0] + lens[1]).astype(F32)
    first = jnp.where(lane[0:1] == 1, tokens, first)
    for h in range(2):
        rows = (
            gae[h : h + 1], gae[2 + h : 3 + h], returns[h : h + 1], returns[2 + h : 3 + h],
            valid[h : h + 1], valid[2 + h : 3 + h], first, second,
        )
        send3[h] = jnp.concatenate(rows, axis=0)
    recv3[mb] = send3[mb // 4]

    def third_copy(k):
        return pltpu.make_async_remote_copy(
            src_ref=send3.at[batch_peer(k) // 4],
            dst_ref=recv3.at[mb],
            send_sem=ssem.at[2],
            recv_sem=rsem.at[2],
            device_id={"batch": batch_peer(k)},
            device_id_type=MESH,
        )

    for k in range(1, NB):
        third_copy(k).start()
    arrived(recv3, NB - 1, rsem.at[2])
    got = recv3[...]
    sums = jnp.sum(got, axis=0)
    count = sums[6:7, 1:2]
    mean = (sums[6:7, 0:1] + sums[6:7, 64:65]) / count
    var = jnp.maximum((sums[7:8, 0:1] + sums[7:8, 64:65]) / count - mean * mean, 1.0)
    scale = lax.rsqrt(var)
    rows = lambda k: got[:, k : k + 2, :].reshape(2 * NB, 128)
    advantages = (rows(0) - mean) * rows(4) * scale
    back = lax.rem(128 - lax.rem(mb, 4) * 32, 128)
    adv_ref[...] = pltpu.roll(advantages, back, 1)[:, 0:32]
    ret_ref[...] = pltpu.roll(rows(2), back, 1)[:, 0:32]

    def sent(buffer, count, sem):
        whole = buffer.at[pl.ds(0, count)]
        pltpu.make_async_remote_copy(
            src_ref=whole, dst_ref=whole, send_sem=sem, recv_sem=rsem.at[0],
            device_id={"seq": peer(0, 1)}, device_id_type=MESH,
        ).wait_send()

    sent(recv1, NS - 1, ssem.at[0])
    sent(recv2, NS - 1, ssem.at[1])
    sent(recv3, NB - 1, ssem.at[2])


def per_device(hidden, gain, weight, rewards, mask, lengths, horizon):
    responses, tokens, width = hidden.shape
    out = jax.ShapeDtypeStruct((2 * NB, 32), F32)
    return pl.pallas_call(
        kernel,
        name="critic_gae",
        out_shape=(out, out),
        in_specs=[pl.BlockSpec(memory_space=pltpu.HBM)] * 7,
        out_specs=(pl.BlockSpec(memory_space=pltpu.VMEM),) * 2,
        scratch_shapes=[
            pltpu.VMEM(hidden.shape, BF16),
            pltpu.VMEM(gain.shape, F32),
            pltpu.VMEM(weight.shape, F32),
            pltpu.VMEM(rewards.shape, F32),
            pltpu.VMEM(mask.shape, jnp.int32),
            pltpu.SMEM(lengths.shape, jnp.int32),
            pltpu.SMEM(horizon.shape, F32),
            pltpu.VMEM((NS, 8, 128), F32),
            pltpu.VMEM((NS - 1, 8, 128), F32),
            pltpu.VMEM((1, 128), F32),
            pltpu.VMEM((NS, 1, 128), F32),
            pltpu.VMEM((2, 8, 128), F32),
            pltpu.VMEM((NB, 8, 128), F32),
            pltpu.SemaphoreType.DMA((CHUNKS,)),
            pltpu.SemaphoreType.DMA((2,)),
            pltpu.SemaphoreType.DMA((4,)),
            pltpu.SemaphoreType.DMA((3,)),
            pltpu.SemaphoreType.DMA((3,)),
        ],
        compiler_params=pltpu.CompilerParams(collective_id=0, has_side_effects=True),
    )(hidden, gain, weight, rewards, mask, lengths, horizon)


def solution(mesh):
    return jax.shard_map(
        per_device,
        mesh=mesh,
        in_specs=(
            P("batch", None, "seq"), P("seq"), P("seq"), P("batch", "seq"), P("batch", "seq"),
            P("batch"), P("batch"),
        ),
        out_specs=(P(None, ("seq", "batch")), P(None, ("seq", "batch"))),
        check_vma=False,
    )
```

time: 119 us -> 33.8 us (0.28)
  blocking collectives: 43.6 us -> 0 us
  Pallas kernels: 0 us -> 30.3 us
  waiting for transfers between devices: 29.4 us -> 0 us
  starting transfers between devices: 25.8 us -> 0 us
  other arithmetic: 9.9 us -> 0 us
  local copies, waits for them, and re-layouts: 5.74 us -> 2.59 us
  between operations: 3.44 us -> 0.64 us
    psum x4 -> x0, blocking collectives: 43.6 us -> none  [one_axis_at_a_time(): array = lax.psum(array, axis)]
    pallas_call x0 -> x1, Pallas kernels: none -> 30.3 us  [per_device(): pl.pallas_call(kernel, name='critic_gae', out_shape=(out, out), in_specs=...]
    all_to_all x4 -> x0, waiting for transfers between devices: 26.3 us -> none  [the longest x1 8.98 us: sent_and_summed(): lax.all_to_all(cut_along(array, dim, devices), axis, 0, 0, tiled=True)]
    all_to_all x4 -> x0, starting transfers between devices: 24.5 us -> none  [the longest x1 11.9 us: sent_and_summed(): lax.all_to_all(cut_along(array, dim, devices), axis, 0, 0, tiled=True)]
    reduce_sum x3 -> x0, other arithmetic: 7.3 us -> none  [the longest x1 6.65 us: per_device(): part_squares = jnp.sum(wide_rows * wide_rows, -1)]
    ppermute x1 -> x0, waiting for transfers between devices: 3.01 us -> none  [from_behind(): lax.ppermute(value, axis, [(source, source + steps) for source in range(i...]
    slice x26 -> x0, local copies, waits for them, and re-layouts: 2.44 us -> none  [the longest x20 1.95 us: joined_by_halves(): part[side::2]]
    mul x9 -> x0, other arithmetic: 1.57 us -> none  [the longest x1 0.7 us: per_device(): part_projected = jnp.sum(wide_rows * (gain * value_weight), -1)]
  transfers between devices with their start and end apart: 5 -> 0, of which waited for: 5 -> 0; matrix products, arithmetic and copies ran while one was open for 1% -> 0% of each run, Pallas kernels for 0% -> 0%
where the time goes in v1:
time: 33.8 us; the launch traced here: 33.6 us
  Pallas kernels  30.3 us (90%)
  local copies, waits for them, and re-layouts  2.59 us (8%)
  between operations  0.64 us (2%)
    pallas_call x1, Pallas kernels, per_device(): pl.pallas_call(kernel, name='critic_gae', out_shape=(out, out), in_specs=...  30.3 us
    unnamed x2, local copies, waits for them, and re-layouts  2.59 us

profile of v1, /device:TPU:1, one launch (start us, length us, event | category | flops | bytes accessed | tf_op | source)
XLA Modules:
  0.0 33.6 jit_solution(5206221001451104430)
XLA Ops:
  0.6 30.3 %critic_gae.1 = (f32[16,32]{1,0:T(8,128)}, f32[16,32]{1,0:T(8,128)}) custom-call(bf16[2,8192,128]{2,1,0:T(8,128)(2,1)} %hidden.1, f32[128]{0:T(128)} %gain.1, f32[128]{0:T(128)} %weight.1, f32[2,256]{1,0:T(2,128)} %rewards.1, s32[2,256]{1,0:T(2,128)} %mask.1, s32[2]{0:T(128)} %lengths.1, f32[2]{0:T(128)} %horizon.1), custom_call_target="tpu_custom_call" | custom-call | tf_op jit(solution)/shard_map/critic_gae/pallas_call | solution.py:280
  31.0 1.3 %copy.11 = f32[16,32]{1,0:T(8,128)} copy(f32[16,32]{1,0:T(8,128)} %get-tuple-element.4) | data formatting | bytes 4096
  32.3 1.3 %copy.12 = f32[16,32]{1,0:T(8,128)} copy(f32[16,32]{1,0:T(8,128)} %get-tuple-element.5) | data formatting | bytes 4096
